TPU v7x, 32 devices: a whole 2x2x4 slice. The times are simulated.
32 devices in a mesh: grp: 4 (over y, x), seq: 8 (over z, core).
Axes of the slice: x: 2, y: 2, z: 4, core: 2. Of those that a mesh axis runs over, the one named last changes fastest.
Arguments:
- tokens: bfloat16 [2048, 8192], P(None, 'seq'), may hold values from -16 to 16
- proj_weight: bfloat16 [8192, 5120], P('seq', 'grp'), may hold values from -0.0625 to 0.0625
- proj_bias: bfloat16 [5120], P('grp'), may hold values from -3 to 3
- out_weight: bfloat16 [4096, 8192], P('grp'), may hold values from -0.125 to 0.125
- doc_ids: int32 [2048], P('seq'), may hold values from 0 to 2, never falling along the last dimension, each value on 1 to 1280 neighbouring positions
Outputs:
- mixed: bfloat16 [2048, 8192], P('seq', 'grp')
Inputs may be any that keep to these rules, and one draw needn't show every extreme that they name: `doc_ids`: numbers never fall along the sequence; every document has 1 to 1280 tokens, one exactly that many; every number up to 2 is used.
All inputs are finite; a program needn't handle non-finite values.
Results may differ from a plain program's by a relative error of at most 0.012.
Values may be sent and summed in bfloat16 or wider, within the bound.
A program may use at most 256 MiB of HBM per device.

v0:
```python
import jax
import jax.numpy as jnp
from jax import lax
from jax.sharding import PartitionSpec as P

HEAD_DIM = 128
GQA = 8
theta_base = 1000000.0
neg_large = -1e30


def rotate(inputs, positions, head_dim):
    half_dim = head_dim // 2
    inverse_freq = theta_base ** (-(jnp.arange(half_dim, dtype=jnp.float32) * 2.0) / head_dim)
    angles = positions.astype(jnp.float32)[:, None] * inverse_freq[None, :]
    cosine = jnp.concatenate([jnp.cos(angles), jnp.cos(angles)], axis=1)
    sine_table = jnp.concatenate([jnp.sin(angles), jnp.sin(angles)], axis=1)
    low_half = inputs[..., :half_dim]
    high_half = inputs[..., half_dim:]
    turned = jnp.concatenate([-high_half, low_half], axis=-1)
    return inputs * cosine[:, None, :] + turned * sine_table[:, None, :]


def body(tokens, proj_weight, proj_bias, out_weight, doc_ids):
    tok_rows = doc_ids.shape[0]
    kv_local = proj_weight.shape[1] // ((GQA + 2) * HEAD_DIM)
    my_start = lax.axis_index("seq") * tok_rows
    projected = lax.psum_scatter(
        jnp.dot(tokens, proj_weight, preferred_element_type=jnp.float32),
        "seq",
        scatter_dimension=0,
        tiled=True,
    )
    projected = projected + proj_bias.astype(jnp.float32)[None, :]
    projected = projected.reshape(tok_rows, kv_local, GQA + 2, HEAD_DIM)
    positions = my_start + jnp.arange(tok_rows, dtype=jnp.int32)
    queries = rotate(
        projected[:, :, :GQA, :].reshape(tok_rows, kv_local * GQA, HEAD_DIM), positions, HEAD_DIM
    )
    queries = queries.astype(jnp.bfloat16).reshape(tok_rows, kv_local, GQA, HEAD_DIM)
    key_rows = rotate(projected[:, :, GQA, :], positions, HEAD_DIM).astype(jnp.bfloat16)
    value_rows = projected[:, :, GQA + 1, :].astype(jnp.bfloat16)
    score_scale = HEAD_DIM ** (-0.5)
    initial = (
        jnp.full((kv_local, GQA, tok_rows), neg_large, jnp.float32),
        jnp.zeros((kv_local, GQA, tok_rows), jnp.float32),
        jnp.zeros((kv_local, GQA, tok_rows, HEAD_DIM), jnp.float32),
    )
    key_block = lax.all_gather(key_rows, "seq", axis=0, tiled=True)
    value_block = lax.all_gather(value_rows, "seq", axis=0, tiled=True)
    block_ids = lax.all_gather(doc_ids, "seq", axis=0, tiled=True)
    key_index = jnp.arange(block_ids.shape[0], dtype=jnp.int32)
    allowed = (
        (block_ids[None, :] == doc_ids[:, None])
        & (key_index[None, :] <= positions[:, None])
        & (key_index[None, :] >= 0)
    )

    def compute(state):
        row_max, row_sum, weighted = state
        scores = (
            jnp.einsum("qkgd,pkd->kgqp", queries, key_block, preferred_element_type=jnp.float32)
            * score_scale
        )
        scores = jnp.where(allowed[None, None], scores, neg_large)
        new_max = jnp.maximum(row_max, jnp.max(scores, axis=-1))
        weights = jnp.where(allowed[None, None], jnp.exp(scores - new_max[..., None]), 0.0)
        new_sum = jnp.sum(weights, axis=-1)
        update = jnp.einsum(
            "kgqp,pkd->kgqd",
            weights.astype(jnp.bfloat16),
            value_block,
            preferred_element_type=jnp.float32,
        )
        return (new_max, new_sum, update)

    folded = lax.cond(jnp.any(allowed), compute, lambda state: state, initial)
    row_max, row_sum, weighted = folded
    outputs = (weighted / row_sum[..., None]).astype(jnp.bfloat16)
    attended = jnp.transpose(outputs, (2, 0, 1, 3)).reshape(tok_rows, kv_local * GQA * HEAD_DIM)
    partial_value = jnp.dot(attended, out_weight, preferred_element_type=jnp.float32)
    return lax.psum_scatter(partial_value, "grp", scatter_dimension=1, tiled=True).astype(
        jnp.bfloat16
    )


def solution(mesh):
    return jax.shard_map(
        body,
        mesh=mesh,
        in_specs=(P(None, "seq"), P("seq", "grp"), P("grp"), P("grp", None), P("seq")),
        out_specs=P("seq", "grp"),
        check_vma=False,
    )
```

profile of v0, /device:TPU:0, one launch (start us, length us, event | category | flops | bytes accessed | tf_op | source)
XLA Modules:
  0.0 283.6 jit_solution(13679033153051287310)
XLA Ops:
  6.5 0.0 copy-start
  6.5 0.0 reduce-scatter.3.cloned.1.call-start
  6.5 1.7 copy-done
  8.3 9.7 %fusion.27 = f32[2048,1280]{1,0:T(8,128)} fusion(bf16[2048,1024]{1,0:T(8,128)(2,1)} %param.7, bf16[1024,1280]{1,0:T(8,128)(2,1)S(1)} %copy-done), kind=kOutput, calls=%fused_computation.45 | convolution fusion | flops 5368709120 | bytes 17301504 | tf_op jit(solution)/shard_map/dot_general | solution.py:29
  18.0 0.0 copy-start.3
  18.0 0.0 copy-start.2
  18.0 0.0 reduce-scatter.3.cloned.1.call-update
  18.0 0.0 reduce-scatter.5.cloned.1.call-start
  18.0 0.6 copy-done.3
  18.6 0.0 copy-done.2
  18.7 13.5 %all-gather.1 = s32[8,1,256]{2,1,0:T(1,128)S(1)} all-gather(s32[1,1,256]{2,1,0:T(1,128)S(1)} %bitcast.80), channel_id=1, replica_groups=mesh['grp'=4,'seq'=8] {'seq'}, dimensions={0}, use_global_device_ids=true | all-gather | bytes 9216 | tf_op jit(solution)/shard_map/all_gather | solution.py:51
  32.1 1.2 fusion.17
  34.0 0.3 multiply_cosine_fusion
  34.4 95.8 %reduce-scatter.3.cloned.1.call-done = f32[256,1280]{1,0:T(8,128)} async-done(((f32[2048,1280]{1,0:T(8,128)}), f32[256,1280]{1,0:T(8,128)}) %reduce-scatter.3.cloned.1.call-update) | async-done | bytes 1310736 | tf_op jit(solution)/shard_map/reduce_scatter | solution.py:28
  130.2 2.5 broadcast_add_fusion
  132.7 1.7 copy.17
  134.4 0.1 slice_bitcast_fusion
  134.6 14.8 %all_gather.10 = bf16[2048,1,128]{0,2,1:T(8,128)(2,1)S(1)} all-gather(bf16[256,1,128]{0,2,1:T(8,128)(2,1)S(1)} %fusion.22), channel_id=1, replica_groups=mesh['grp'=4,'seq'=8] {'seq'}, dimensions={0}, use_global_device_ids=true | all-gather | bytes 589824 | tf_op jit(solution)/shard_map/all_gather | solution.py:49
  149.4 14.9 %all-gather = bf16[2048,1,1,128]{0,3,2,1:T(8,128)(2,1)S(1)} all-gather(bf16[256,1,1,128]{0,3,2,1:T(8,128)(2,1)S(1)} %slice.47), channel_id=2, replica_groups=mesh['grp'=4,'seq'=8] {'seq'}, dimensions={0}, use_global_device_ids=true | all-gather | bytes 589824 | tf_op jit(solution)/shard_map/all_gather | solution.py:50
  164.3 0.1 fusion.20
  164.4 0.2 fusion.19
  164.6 11.5 %conditional.1 = (f32[1,8,256]{2,1,0:T(8,128)S(1)}, f32[1,8,256,128]{2,3,1,0:T(8,128)S(1)}) conditional(s32[]{:T(128)} %convert_element_type.50, () %tuple.13, (pred[256,2048]{0,1:T(8,128)(4,1)S(1)}, bf16[2048,1,128]{0,2,1:T(8,128)(2,1)S(1)}, bf16[256,1,8,128]{0,3,2,1:T(8,128)(2,1)S(1)}, bf16[2048,1,128]{0,2,1:T(8,128)(2,1)S(1)}) %tuple.33), branch_computations={%region_2.0_spmd, %region_3.6_spmd} | conditional | flops 2202007552 | bytes 54575120 | solution.py:77
  164.6 2.7 fusion
  167.4 4.0 %fusion.2 = f32[8,256]{1,0:T(8,128)S(1)} fusion(f32[2048,256,8]{1,0,2:T(8,128)S(1)} %get-tuple-element.31, f32[8,256]{1,0:T(8,128)S(1)} %broadcast_maximum_fusion, pred[256,2048]{0,1:T(8,128)(4,1)S(1)} %get-tuple-element.13), kind=kLoop, calls=%fused_computation.4 | loop fusion | flops 20969472 | bytes 17317888 | tf_op jit(solution)/shard_map/cond/branch_1_fun/reduce_sum | solution.py:68
  171.4 4.5 %fusion.7 = f32[1,8,256,128]{2,3,1,0:T(8,128)S(1)} fusion(f32[2048,256,8]{1,0,2:T(8,128)S(1)} %get-tuple-element.31, f32[8,256]{1,0:T(8,128)S(1)} %broadcast_maximum_fusion, pred[256,2048]{0,1:T(8,128)(4,1)S(1)} %get-tuple-element.13, bf16[2048,1,128]{0,2,1:T(8,128)(2,1)S(1)} %get-tuple-element.28), kind=kOutput, calls=%fused_computation.8 | convolution fusion | flops 1094713344 | bytes 18882560 | tf_op jit(solution)/shard_map/cond/branch_1_fun/kgqp,pkd->kgqd/dot_general | solution.py:69
  176.1 0.1 divide_convert_fusion
  176.2 0.0 copy-start.1
  176.2 12.9 %fusion.28 = f32[256,8192]{1,0:T(8,128)} fusion(bf16[256,1024]{0,1:T(8,128)(2,1)S(1)} %bitcast.75, bf16[1024,8192]{1,0:T(8,128)(2,1)} %param.10), kind=kOutput, calls=%fused_computation.46 | convolution fusion | flops 4294967296 | bytes 25690112 | tf_op jit(solution)/shard_map/dot_general | solution.py:81
  189.1 0.0 reduce-scatter.5.cloned.1.call-update
  189.1 85.0 %reduce-scatter.5.cloned.1.call-done = f32[256,2048]{1,0:T(8,128)} async-done(((f32[256,8192]{1,0:T(8,128)}), f32[256,2048]{1,0:T(8,128)}) %reduce-scatter.5.cloned.1.call-update) | async-done | bytes 2097168 | tf_op jit(solution)/shard_map/reduce_scatter | solution.py:82
  274.1 2.7 convert_element_type.57
  276.8 0.0 copy-done.1
  (10 shorter events, 0.1 us)
Async XLA Ops:
  6.5 1.7 copy-start
  6.5 123.7 %reduce-scatter.3.cloned.1.call-start = ((), (), s32[]{:S(2)}) async-start(), calls=%async_computation.2 | async-start | bytes 11796480 | tf_op jit(solution)/shard_map/reduce_scatter | solution.py:28
  18.0 0.7 copy-start.3
  18.0 0.7 copy-start.2
  18.0 256.1 %reduce-scatter.5.cloned.1.call-start = ((), (), s32[]{:S(2)}) async-start(), calls=%async_computation.3 | async-start | bytes 10485760 | tf_op jit(solution)/shard_map/reduce_scatter | solution.py:82
  176.2 100.6 %copy-start.1 = (bf16[1024,1280]{1,0:T(8,128)(2,1)S(1)}, bf16[1024,1280]{1,0:T(8,128)(2,1)}, u32[]{:S(2)}) copy-start(bf16[1024,1280]{1,0:T(8,128)(2,1)} %param.8) | copy-start | bytes 7864324
Sparse Core Ops, SparseCore 0:
  18.1 112.0 reduce-scatter.2
  189.2 84.8 reduce-scatter.4
where the time goes:
time: 284 us
  waiting for transfers between devices  181 us (64%)
  blocking collectives  43.2 us (15%)
  matrix products  29.8 us (10%)
  between operations  14.2 us (5%)
  other arithmetic  11.2 us (4%)
  local copies, waits for them, and re-layouts  4.16 us (1%)
    reduce_scatter x1, waiting for transfers between devices, body(): lax.psum_scatter(jnp.dot(tokens, proj_weight, preferred_element_type=jnp....  95.8 us
    reduce_scatter x1, waiting for transfers between devices, body(): lax.psum_scatter(partial_value, 'grp', scatter_dimension=1, tiled=True)  85 us
    all_gather x1, blocking collectives, body(): value_block = lax.all_gather(value_rows, 'seq', axis=0, tiled=True)  14.9 us
    all_gather x1, blocking collectives, body(): key_block = lax.all_gather(key_rows, 'seq', axis=0, tiled=True)  14.8 us
    all_gather x1, blocking collectives, body(): block_ids = lax.all_gather(doc_ids, 'seq', axis=0, tiled=True)  13.5 us
    dot_general x1, matrix products, body(): jnp.dot(attended, out_weight, preferred_element_type=jnp.float32)  12.9 us
    dot_general x1, matrix products, body(): jnp.dot(tokens, proj_weight, preferred_element_type=jnp.float32)  9.68 us
  transfers between devices with their start and end apart: 2, of which 2 were waited for; matrix products, arithmetic and copies ran while one was open for 1% of the time, Pallas kernels for 0%

commit v1 on v0

--- a/solution.py
+++ b/solution.py
@@ -1,12 +1,37 @@
+import functools
 import jax
 import jax.numpy as jnp
 from jax import lax
 from jax.sharding import PartitionSpec as P
+from jax.lax import axis_index, axis_size, ppermute
 
 HEAD_DIM = 128
 GQA = 8
 theta_base = 1000000.0
 neg_large = -1e30
+
+
+def view_press(block_here, lane_axis):
+    n = axis_size(lane_axis)
+    u = 0
+    blocks_here = []
+    while u < n:
+        blocks_here.append((u, (u + 1) % n))
+        u = u + 1
+
+    def flows_post(carry_out):
+        if len(carry_out) == n:
+            return carry_out
+        return flows_post([ppermute(carry_out[0], lane_axis, blocks_here), *carry_out])
+
+    return jnp.roll(
+        jnp.concatenate(flows_post([block_here]), axis=0),
+        (axis_index(lane_axis) + 1) * block_here.shape[0],
+        0,
+    )
+
+
+get_paths = functools.partial(view_press, lane_axis="seq")
 
 
 def rotate(inputs, positions, head_dim):
@@ -46,7 +71,7 @@
         jnp.zeros((kv_local, GQA, tok_rows), jnp.float32),
         jnp.zeros((kv_local, GQA, tok_rows, HEAD_DIM), jnp.float32),
     )
-    key_block = lax.all_gather(key_rows, "seq", axis=0, tiled=True)
+    key_block = get_paths(key_rows)
     value_block = lax.all_gather(value_rows, "seq", axis=0, tiled=True)
     block_ids = lax.all_gather(doc_ids, "seq", axis=0, tiled=True)
     key_index = jnp.arange(block_ids.shape[0], dtype=jnp.int32)

time: 284 us -> 311 us (1.095)
  waiting for transfers between devices: 181 us -> 213 us
  blocking collectives: 43.2 us -> 28.3 us
  local copies, waits for them, and re-layouts: 4.16 us -> 14.6 us
    ppermute x0 -> x7, waiting for transfers between devices: none -> 30.6 us  [flows_post(): ppermute(carry_out[0], lane_axis, blocks_here)]
    all_gather x1 -> x0, blocking collectives: 14.8 us -> none  [body(): key_block = lax.all_gather(key_rows, 'seq', axis=0, tiled=True)]
    unnamed x8 -> x23, local copies, waits for them, and re-layouts: 2.36 us -> 11.9 us
  transfers between devices with their start and end apart: 2 -> 9, of which waited for: 2 -> 8; matrix products, arithmetic and copies ran while one was open for 1% -> 1% of each run, Pallas kernels for 0% -> 0%
where the time goes in v1:
time: 311 us
  waiting for transfers between devices  213 us (68%)
  matrix products  29.7 us (10%)
  blocking collectives  28.3 us (9%)
  local copies, waits for them, and re-layouts  14.6 us (5%)
  between operations  14.2 us (5%)
  other arithmetic  10.2 us (3%)
    reduce_scatter x1, waiting for transfers between devices, body(): lax.psum_scatter(jnp.dot(tokens, proj_weight, preferred_element_type=jnp....  97.7 us
    reduce_scatter x1, waiting for transfers between devices, body(): lax.psum_scatter(partial_value, 'grp', scatter_dimension=1, tiled=True)  84.8 us
    ppermute x7, waiting for transfers between devices, flows_post(): ppermute(carry_out[0], lane_axis, blocks_here)  30.6 us
    all_gather x1, blocking collectives, body(): value_block = lax.all_gather(value_rows, 'seq', axis=0, tiled=True)  14.8 us
    all_gather x1, blocking collectives, body(): block_ids = lax.all_gather(doc_ids, 'seq', axis=0, tiled=True)  13.5 us
    dot_general x1, matrix products, body(): jnp.dot(attended, out_weight, preferred_element_type=jnp.float32)  12.9 us
    unnamed x23, local copies, waits for them, and re-layouts  11.9 us
    dot_general x1, matrix products, body(): jnp.dot(tokens, proj_weight, preferred_element_type=jnp.float32)  9.68 us
  transfers between devices with their start and end apart: 9, of which 8 were waited for; matrix products, arithmetic and copies ran while one was open for 1% of the time, Pallas kernels for 0%

profile of v1, /device:TPU:0, one launch (start us, length us, event | category | flops | bytes accessed | tf_op | source)
XLA Modules:
  0.0 310.5 jit_solution(2219195163523747733)
XLA Ops:
  6.5 1.7 copy-done
  8.3 9.7 %fusion.29 = f32[2048,1280]{1,0:T(8,128)} fusion(bf16[2048,1024]{1,0:T(8,128)(2,1)} %param.7, bf16[1024,1280]{1,0:T(8,128)(2,1)S(1)} %copy-done), kind=kOutput, calls=%fused_computation.63 | convolution fusion | flops 5368709120 | bytes 17301504 | tf_op jit(solution)/shard_map/dot_general | solution.py:54
  18.0 0.0 reduce-scatter.3.cloned.1.call-update
  18.0 0.0 reduce-scatter.5.cloned.1.call-start
  18.0 0.6 copy-done.3
  18.7 13.5 %all-gather.1 = s32[8,1,256]{2,1,0:T(1,128)S(1)} all-gather(s32[1,1,256]{2,1,0:T(1,128)S(1)} %bitcast.86), channel_id=1, replica_groups=mesh['grp'=4,'seq'=8] {'seq'}, dimensions={0}, use_global_device_ids=true | all-gather | bytes 9216 | tf_op jit(solution)/shard_map/all_gather | solution.py:76
  32.1 0.3 multiply_cosine_fusion
  32.5 97.7 %reduce-scatter.3.cloned.1.call-done = f32[256,1280]{1,0:T(8,128)} async-done(((f32[2048,1280]{1,0:T(8,128)}), f32[256,1280]{1,0:T(8,128)}) %reduce-scatter.3.cloned.1.call-update) | async-done | bytes 1310736 | tf_op jit(solution)/shard_map/reduce_scatter | solution.py:53
  130.2 1.4 broadcast_add_fusion
  131.6 0.4 copy.17
  132.1 0.1 collective-permute-start
  132.2 5.5 %collective-permute-done = bf16[256,1,128]{0,2,1:T(8,128)(2,1)S(1)} collective-permute-done((bf16[256,1,128]{0,2,1:T(8,128)(2,1)S(1)}, bf16[256,1,128]{0,2,1:T(8,128)(2,1)S(1)}, u32[]{:S(2)}, u32[]{:S(2)}) %collective-permute-start) | collective-permute-done | bytes 65568 | tf_op jit(solution)/shard_map/ppermute | solution.py:25
  137.6 1.2 fusion.19
  139.5 3.6 %collective-permute-done.1 = bf16[256,1,128]{0,2,1:T(8,128)(2,1)S(1)} collective-permute-done((bf16[256,1,128]{0,2,1:T(8,128)(2,1)S(1)}, bf16[256,1,128]{0,2,1:T(8,128)(2,1)S(1)}, u32[]{:S(2)}, u32[]{:S(2)}) %collective-permute-start.1) | collective-permute-done | bytes 65568 | tf_op jit(solution)/shard_map/ppermute | solution.py:25
  143.1 5.5 %collective-permute-done.2 = bf16[256,1,128]{0,2,1:T(8,128)(2,1)S(1)} collective-permute-done((bf16[256,1,128]{0,2,1:T(8,128)(2,1)S(1)}, bf16[256,1,128]{0,2,1:T(8,128)(2,1)S(1)}, u32[]{:S(2)}, u32[]{:S(2)}) %collective-permute-start.2) | collective-permute-done | bytes 65568 | tf_op jit(solution)/shard_map/ppermute | solution.py:25
  148.6 0.1 slice_bitcast_fusion
  148.7 5.4 %collective-permute-done.3 = bf16[256,1,128]{0,2,1:T(8,128)(2,1)S(1)} collective-permute-done((bf16[256,1,128]{0,2,1:T(8,128)(2,1)S(1)}, bf16[256,1,128]{0,2,1:T(8,128)(2,1)S(1)}, u32[]{:S(2)}, u32[]{:S(2)}) %collective-permute-start.3) | collective-permute-done | bytes 65568 | tf_op jit(solution)/shard_map/ppermute | solution.py:25
  154.1 0.1 fusion.22
  154.2 5.4 %collective-permute-done.4 = bf16[256,1,128]{0,2,1:T(8,128)(2,1)S(1)} collective-permute-done((bf16[256,1,128]{0,2,1:T(8,128)(2,1)S(1)}, bf16[256,1,128]{0,2,1:T(8,128)(2,1)S(1)}, u32[]{:S(2)}, u32[]{:S(2)}) %collective-permute-start.4) | collective-permute-done | bytes 65568 | tf_op jit(solution)/shard_map/ppermute | solution.py:25
  159.6 0.2 fusion.21
  159.8 5.3 %collective-permute-done.5 = bf16[256,1,128]{0,2,1:T(8,128)(2,1)S(1)} collective-permute-done((bf16[256,1,128]{0,2,1:T(8,128)(2,1)S(1)}, bf16[256,1,128]{0,2,1:T(8,128)(2,1)S(1)}, u32[]{:S(2)}, u32[]{:S(2)}) %collective-permute-start.5) | collective-permute-done | bytes 65568 | tf_op jit(solution)/shard_map/ppermute | solution.py:25
  165.1 14.8 %all-gather = bf16[2048,1,1,128]{0,3,2,1:T(8,128)(2,1)S(1)} all-gather(bf16[256,1,1,128]{0,3,2,1:T(8,128)(2,1)S(1)} %slice.47), channel_id=2, replica_groups=mesh['grp'=4,'seq'=8] {'seq'}, dimensions={0}, use_global_device_ids=true | all-gather | bytes 589824 | tf_op jit(solution)/shard_map/all_gather | solution.py:75
  180.0 0.6 constant_dynamic-update-slice_fusion.15
  180.6 0.6 constant_dynamic-update-slice_fusion.14
  181.2 0.6 constant_dynamic-update-slice_fusion.13
  181.9 0.6 constant_dynamic-update-slice_fusion.12
  182.5 0.6 constant_dynamic-update-slice_fusion.11
  183.1 0.6 constant_dynamic-update-slice_fusion.10
  183.8 0.6 constant_dynamic-update-slice_fusion.9
  184.4 0.6 constant_dynamic-update-slice_fusion.8
  185.0 0.6 constant_dynamic-update-slice_fusion.7
  185.7 0.6 constant_dynamic-update-slice_fusion.6
  186.3 0.6 constant_dynamic-update-slice_fusion.5
  187.0 0.6 constant_dynamic-update-slice_fusion.4
  187.6 0.6 constant_dynamic-update-slice_fusion.3
  188.2 0.6 constant_dynamic-update-slice_fusion.2
  188.9 0.6 constant_dynamic-update-slice_fusion.1
  189.5 0.6 constant_dynamic-update-slice_fusion
  190.1 13.0 %conditional.1 = (f32[1,8,256]{2,1,0:T(8,128)S(1)}, f32[1,8,256,128]{2,3,1,0:T(8,128)S(1)}) conditional(s32[]{:T(128)} %convert_element_type.53, () %tuple.24, (pred[256,2048]{0,1:T(8,128)(4,1)S(1)}, s32[]{:T(128)}, bf16[4096,1,128]{0,2,1:T(8,128)(2,1)}, bf16[256,1,8,128]{0,3,2,1:T(8,128)(2,1)S(1)}, bf16[2048,1,128]{0,2,1:T(8,128)(2,1)S(1)}, ...), branch_computations={%region_2.3_spmd, %region_3.6_spmd.clone.clone} | conditional | flops 2202007552 | bytes 56672432 | solution.py:102
  190.1 1.6 copy.25
  191.7 2.7 fusion
  194.4 4.0 %fusion.2 = f32[8,256]{1,0:T(8,128)S(1)} fusion(f32[2048,256,8]{1,0,2:T(8,128)S(1)} %get-tuple-element.164, f32[8,256]{1,0:T(8,128)S(1)} %broadcast_maximum_fusion, pred[256,2048]{0,1:T(8,128)(4,1)S(1)} %get-tuple-element.149), kind=kLoop, calls=%fused_computation.4 | loop fusion | flops 20969472 | bytes 17317888 | tf_op jit(solution)/shard_map/cond/branch_1_fun/reduce_sum | solution.py:93
  198.5 4.5 %fusion.7 = f32[1,8,256,128]{2,3,1,0:T(8,128)S(1)} fusion(f32[2048,256,8]{1,0,2:T(8,128)S(1)} %get-tuple-element.164, f32[8,256]{1,0:T(8,128)S(1)} %broadcast_maximum_fusion, pred[256,2048]{0,1:T(8,128)(4,1)S(1)} %get-tuple-element.149, bf16[2048,1,128]{0,2,1:T(8,128)(2,1)S(1)} %get-tuple-element.152), kind=kOutput, calls=%fused_computation.8 | convolution fusion | flops 1094713344 | bytes 18882560 | tf_op jit(solution)/shard_map/cond/branch_1_fun/kgqp,pkd->kgqd/dot_general | solution.py:94
  203.1 0.1 divide_convert_fusion
  203.2 12.9 %fusion.30 = f32[256,8192]{1,0:T(8,128)} fusion(bf16[256,1024]{0,1:T(8,128)(2,1)S(1)} %bitcast.81, bf16[1024,8192]{1,0:T(8,128)(2,1)} %param.10), kind=kOutput, calls=%fused_computation.64 | convolution fusion | flops 4294967296 | bytes 25690112 | tf_op jit(solution)/shard_map/dot_general | solution.py:106
  216.1 0.0 reduce-scatter.5.cloned.1.call-update
  216.2 84.8 %reduce-scatter.5.cloned.1.call-done = f32[256,2048]{1,0:T(8,128)} async-done(((f32[256,8192]{1,0:T(8,128)}), f32[256,2048]{1,0:T(8,128)}) %reduce-scatter.5.cloned.1.call-update) | async-done | bytes 2097168 | tf_op jit(solution)/shard_map/reduce_scatter | solution.py:107
  301.0 2.7 convert_element_type.60
  (24 shorter events, 0.1 us)
Async XLA Ops:
  6.5 1.7 copy-start
  6.5 123.7 %reduce-scatter.3.cloned.1.call-start = ((), (), s32[]{:S(2)}) async-start(), calls=%async_computation.2 | async-start | bytes 11796480 | tf_op jit(solution)/shard_map/reduce_scatter | solution.py:53
  18.0 0.7 copy-start.3
  18.0 0.7 copy-start.2
  18.0 283.0 %reduce-scatter.5.cloned.1.call-start = ((), (), s32[]{:S(2)}) async-start(), calls=%async_computation.3 | async-start | bytes 10485760 | tf_op jit(solution)/shard_map/reduce_scatter | solution.py:107
  132.1 5.5 %collective-permute-start = (bf16[256,1,128]{0,2,1:T(8,128)(2,1)S(1)}, bf16[256,1,128]{0,2,1:T(8,128)(2,1)S(1)}, u32[]{:S(2)}, u32[]{:S(2)}) collective-permute-start(bf16[256,1,128]{0,2,1:T(8,128)(2,1)S(1)} %fusion.24), channel_id=1, source_target_pairs={{0,1},{1,2},{2,3},{3,4},{4,5},{5,6},{6,7},{7,0},{8,9},{9,10},{10,1... | collective-permute-start | bytes 196616 | tf_op jit(solution)/shard_map/ppermute | solution.py:25
  137.6 5.5 %collective-permute-start.1 = (bf16[256,1,128]{0,2,1:T(8,128)(2,1)S(1)}, bf16[256,1,128]{0,2,1:T(8,128)(2,1)S(1)}, u32[]{:S(2)}, u32[]{:S(2)}) collective-permute-start(bf16[256,1,128]{0,2,1:T(8,128)(2,1)S(1)} %collective-permute-done), channel_id=1, source_target_pairs={{0,1},{1,2},{2,3},{3,4},{4,5},{5,6},{6,7},{7,0},{8,9},{9,10},{10,1... | collective-permute-start | bytes 196616 | tf_op jit(solution)/shard_map/ppermute | solution.py:25
  143.1 5.5 %collective-permute-start.2 = (bf16[256,1,128]{0,2,1:T(8,128)(2,1)S(1)}, bf16[256,1,128]{0,2,1:T(8,128)(2,1)S(1)}, u32[]{:S(2)}, u32[]{:S(2)}) collective-permute-start(bf16[256,1,128]{0,2,1:T(8,128)(2,1)S(1)} %collective-permute-done.1), channel_id=1, source_target_pairs={{0,1},{1,2},{2,3},{3,4},{4,5},{5,6},{6,7},{7,0},{8,9},{9,10},{10,1... | collective-permute-start | bytes 196616 | tf_op jit(solution)/shard_map/ppermute | solution.py:25
  148.6 5.5 %collective-permute-start.3 = (bf16[256,1,128]{0,2,1:T(8,128)(2,1)S(1)}, bf16[256,1,128]{0,2,1:T(8,128)(2,1)S(1)}, u32[]{:S(2)}, u32[]{:S(2)}) collective-permute-start(bf16[256,1,128]{0,2,1:T(8,128)(2,1)S(1)} %collective-permute-done.2), channel_id=1, source_target_pairs={{0,1},{1,2},{2,3},{3,4},{4,5},{5,6},{6,7},{7,0},{8,9},{9,10},{10,1... | collective-permute-start | bytes 196616 | tf_op jit(solution)/shard_map/ppermute | solution.py:25
  154.1 5.5 %collective-permute-start.4 = (bf16[256,1,128]{0,2,1:T(8,128)(2,1)S(1)}, bf16[256,1,128]{0,2,1:T(8,128)(2,1)S(1)}, u32[]{:S(2)}, u32[]{:S(2)}) collective-permute-start(bf16[256,1,128]{0,2,1:T(8,128)(2,1)S(1)} %collective-permute-done.3), channel_id=1, source_target_pairs={{0,1},{1,2},{2,3},{3,4},{4,5},{5,6},{6,7},{7,0},{8,9},{9,10},{10,1... | collective-permute-start | bytes 196616 | tf_op jit(solution)/shard_map/ppermute | solution.py:25
  159.6 5.5 %collective-permute-start.5 = (bf16[256,1,128]{0,2,1:T(8,128)(2,1)S(1)}, bf16[256,1,128]{0,2,1:T(8,128)(2,1)S(1)}, u32[]{:S(2)}, u32[]{:S(2)}) collective-permute-start(bf16[256,1,128]{0,2,1:T(8,128)(2,1)S(1)} %collective-permute-done.4), channel_id=1, source_target_pairs={{0,1},{1,2},{2,3},{3,4},{4,5},{5,6},{6,7},{7,0},{8,9},{9,10},{10,1... | collective-permute-start | bytes 196616 | tf_op jit(solution)/shard_map/ppermute | solution.py:25
  165.1 14.8 %collective-permute-start.6 = (bf16[256,1,128]{0,2,1:T(8,128)(2,1)S(1)}, bf16[256,1,128]{0,2,1:T(8,128)(2,1)S(1)}, u32[]{:S(2)}, u32[]{:S(2)}) collective-permute-start(bf16[256,1,128]{0,2,1:T(8,128)(2,1)S(1)} %collective-permute-done.5), channel_id=1, source_target_pairs={{0,1},{1,2},{2,3},{3,4},{4,5},{5,6},{6,7},{7,0},{8,9},{9,10},{10,1... | collective-permute-start | bytes 196616 | tf_op jit(solution)/shard_map/ppermute | solution.py:25
  203.2 100.5 %copy-start.1 = (bf16[1024,1280]{1,0:T(8,128)(2,1)S(1)}, bf16[1024,1280]{1,0:T(8,128)(2,1)}, u32[]{:S(2)}) copy-start(bf16[1024,1280]{1,0:T(8,128)(2,1)} %param.8) | copy-start | bytes 7864324
Sparse Core Ops, SparseCore 0:
  18.1 112.0 reduce-scatter.2
  216.3 84.6 reduce-scatter.4
